TPU v7x, 32 devices: a whole 2x2x4 slice. The times are simulated.
32 devices in a mesh: dp: 8 (over z, x), mp: 4 (over y, core).
Axes of the slice: x: 2, y: 2, z: 4, core: 2. Of those that a mesh axis runs over, the one named last changes fastest.
Arguments:
- features: bfloat16 [2048, 512], P('dp'), may hold values from -6 to 6
- adjacency: bfloat16 [64, 32, 128, 128], P('dp'), may hold values from -0.125 to 0.125
- source_block: int32 [64, 32], P('dp'), may hold values from 0 to 1
- edge_type: int32 [64, 32], P('dp'), may hold values from 0 to 19
- target_block: int32 [64, 32], P('dp'), may hold values from 0 to 1
- live_count: int32 [8, 8], P('dp'), may hold values from 24 to 32, as said below
- relation_weight: bfloat16 [20, 512, 512], P(None, None, 'mp'), may hold values from -0.25 to 0.25
- self_weight: bfloat16 [512, 512], P(None, 'mp'), may hold values from -0.25 to 0.25
- layer_bias: bfloat16 [512], P('mp'), may hold values from -3 to 3
- norm_gain: bfloat16 [512], replicated, may hold values from 0.5 to 1.5
Outputs:
- node_states: bfloat16 [2048, 512], P(('dp', 'mp'))
Inputs may be any that keep to these rules, and one draw needn't show every extreme that they name: `source_block`: row s * 8 + d names a block among sender s's 2 blocks. `target_block`: row d * 8 + s names a block among receiver d's 2 blocks. live_count[d, s] live slots from sender s to receiver d, the first ones; some receiver has all 32 slots live from every sender.
All inputs are finite; a program needn't handle non-finite values.
Results may differ from a plain program's by a relative error of at most 0.007.
Values may be sent and summed in bfloat16 or wider, within the bound.
No kernel may reach another device: no remote copies, remote signals or barrier semaphores. Data moves between devices by JAX's collectives and lax.ppermute only.
A program may use at most 128 MiB of HBM per device.

v0:
```python
import jax
import jax.numpy as jnp
from jax import lax
from jax.sharding import PartitionSpec as P

BLK = 128


epsilon = 1e-05


def block_table(features, relation_weight, blocks):
    stacked = features.reshape(blocks, BLK, features.shape[1])
    lookup = jnp.einsum(
        "bid,rdc->bric", stacked, relation_weight, preferred_element_type=jnp.float32
    )
    return lookup.astype(jnp.bfloat16).reshape(
        blocks * relation_weight.shape[0], BLK, relation_weight.shape[2]
    )


def transform_slots(lookup, lookup_rows, adj_tiles):
    chosen = jnp.take(lookup, lookup_rows, axis=0)
    return jnp.einsum("nij,njc->nic", adj_tiles, chosen, preferred_element_type=jnp.float32)


def selector(targets, counts, blocks):
    slot_count = targets.shape[1]
    active = jnp.arange(slot_count, dtype=jnp.int32)[None, :] < counts[:, None]
    matches = targets[:, :, None] == jnp.arange(blocks, dtype=jnp.int32)[None, None, :]
    return jnp.logical_and(matches, active[:, :, None]).astype(jnp.float32)


def per_device(
    features,
    adjacency,
    source_block,
    edge_type,
    target_block,
    live_count,
    relation_weight,
    self_weight,
    layer_bias,
    norm_gain,
):
    peer_count = lax.axis_size("dp")
    slot_count = source_block.shape[1]
    node_rows = features.shape[0]
    blocks = node_rows // BLK
    columns = relation_weight.shape[2]
    lookup = block_table(features, relation_weight, blocks)
    lookup_rows = (source_block * relation_weight.shape[0] + edge_type).reshape(
        peer_count * slot_count
    )
    flat_tiles = adjacency.reshape(peer_count * slot_count, BLK, BLK)
    routed, routed_count = (
        lax.all_to_all(target_block, "dp", split_axis=0, concat_axis=0, tiled=True),
        lax.all_to_all(
            live_count.reshape(peer_count, 1), "dp", split_axis=0, concat_axis=0, tiled=True
        ),
    )
    weights = selector(routed, routed_count[:, 0], blocks)
    receivers = node_rows * lax.axis_size("dp") // node_rows
    message = transform_slots(lookup, lookup_rows, flat_tiles).reshape(
        receivers, slot_count, BLK * columns
    )
    summed = jnp.einsum("rkb,rkx->rbx", weights, message, precision=lax.Precision.HIGHEST)
    aggregate = lax.psum_scatter(
        summed.reshape(receivers * blocks * BLK, columns), "dp", scatter_dimension=0, tiled=True
    )
    own_term = jnp.dot(features, self_weight, preferred_element_type=jnp.float32)
    hidden = jax.nn.relu(own_term + aggregate + layer_bias.astype(jnp.float32)).astype(jnp.bfloat16)
    by_rows = lax.all_to_all(hidden, "mp", split_axis=0, concat_axis=1, tiled=True)
    values = by_rows.astype(jnp.float32)
    inverse_rms = lax.rsqrt(jnp.mean(values * values, axis=1, keepdims=True) + epsilon)
    return (values * inverse_rms * norm_gain.astype(jnp.float32)).astype(jnp.bfloat16)


def solution(mesh):
    return jax.shard_map(
        per_device,
        mesh=mesh,
        in_specs=(
            P("dp", None),
            P("dp", None, None, None),
            P("dp", None),
            P("dp", None),
            P("dp", None),
            P("dp", None),
            P(None, None, "mp"),
            P(None, "mp"),
            P("mp"),
            P(),
        ),
        out_specs=P(("dp", "mp"), None),
        check_vma=False,
    )
```

profile of v0, /device:TPU:0, one launch (start us, length us, event | category | flops | bytes accessed | tf_op | source)
XLA Modules:
  0.0 182.4 jit_solution(16302394386973971121)
XLA Ops:
  6.5 1.5 copy.24
  8.0 7.3 %all-to-all-start.1 = ((s32[8,1,1]{2,1,0:T(1,128)}), s32[8,1,1]{2,1,0:T(1,128)S(1)}, u32[]{:S(2)}, u32[]{:S(2)}) async-start(s32[8,1,1]{2,1,0:T(1,128)} %copy.24), calls=%async_computation.1 | async-start | bytes 8192 | tf_op jit(solution)/shard_map/all_to_all | solution.py:58
  15.3 0.7 multiply_add_fusion
  16.0 0.1 reshape.104
  16.1 0.1 reshape.101
  16.2 2.9 %fusion.8 = bf16[2,20,128,128]{2,3,0,1:T(8,128)(2,1)} fusion(bf16[2,128,512,1]{2,1,0,3:T(8,128)(2,1)} %bitcast.40, bf16[20,512,128]{2,1,0:T(8,128)(2,1)S(1)} %copy-done), kind=kOutput, calls=%fused_computation.8 | convolution fusion | flops 671744000 | bytes 4194304 | tf_op jit(solution)/shard_map/bid,rdc->bric/dot_general | solution.py:14
  19.1 1.8 copy.26
  20.9 8.6 %gather_fusion = bf16[256,128,128]{2,1,0:T(8,128)(2,1)} fusion(bf16[40,128,128]{2,1,0:T(8,128)(2,1)S(1)} %bitcast.38, s32[1024]{0:T(1024)S(1)} %pad_clamp_fusion), kind=kCustom, calls=%fused_computation | custom fusion | bytes 16778240 | tf_op jit(solution)/shard_map/jit(_take)/gather | solution.py:23
  29.5 13.2 %convolution_bitcast_fusion = f32[256,128,128]{1,2,0:T(8,128)} fusion(bf16[256,128,128]{2,1,0:T(8,128)(2,1)} %bitcast.39, bf16[256,128,128]{2,1,0:T(8,128)(2,1)} %gather_fusion, pred[256]{0:T(512)(128)(4,1)S(1)} %compare_and_fusion), kind=kOutput, calls=%fused_computation.1 | convolution fusion | flops 1077936128 | bytes 33554688 | tf_op jit(solution)/shard_map/nij,njc->nic/dot_general | solution.py:24
  42.7 17.4 %copy.28 = f32[256,128,128]{2,1,0:T(8,128)} copy(f32[256,128,128]{1,2,0:T(8,128)} %convolution_bitcast_fusion) | data formatting | bytes 33554432 | tf_op jit(solution)/shard_map/nij,njc->nic/dot_general | solution.py:24
  60.2 18.2 %reshape.106 = f32[8,32,16384]{2,1,0:T(8,128)} reshape(f32[256,128,128]{2,1,0:T(8,128)} %copy.28) | data formatting | bytes 33554432 | tf_op jit(solution)/shard_map/reshape | solution.py:64
  78.4 6.0 %all-to-all-start = ((s32[8,1,32]{2,1,0:T(1,128)}), s32[8,1,32]{2,1,0:T(1,128)S(1)}, u32[]{:S(2)}, u32[]{:S(2)}) async-start(s32[8,1,32]{2,1,0:T(1,128)} %bitcast), calls=%async_computation | async-start | bytes 8192 | tf_op jit(solution)/shard_map/all_to_all | solution.py:57
  84.4 0.0 reduce-scatter.2.cloned.1.call-start
  84.4 0.2 reduce.2
  84.6 0.1 iota_compare_fusion
  84.7 6.1 %all-to-all-done = s32[8,1,32]{2,1,0:T(1,128)S(1)} async-done(((s32[8,1,32]{2,1,0:T(1,128)}), s32[8,1,32]{2,1,0:T(1,128)S(1)}, u32[]{:S(2)}, u32[]{:S(2)}) %all-to-all-start) | async-done | bytes 1056 | tf_op jit(solution)/shard_map/all_to_all | solution.py:57
  90.8 10.0 %fusion.17 = f32[8,2,16384]{2,1,0:T(2,128)} fusion(f32[8,32,16384]{2,1,0:T(8,128)} %reshape.106, pred[8,32]{1,0:T(8,128)(4,1)S(1)} %iota_compare_fusion, s32[8,32]{1,0:T(8,128)S(1)} %bitcast.41), kind=kOutput, calls=%fused_computation.19 | convolution fusion | flops 100664320 | bytes 17827072 | tf_op jit(solution)/shard_map/rkb,rkx->rbx/dot_general | solution.py:67
  100.8 3.1 %reshape.107 = f32[2048,128]{1,0:T(8,128)} reshape(f32[8,2,16384]{2,1,0:T(2,128)} %fusion.17) | data formatting | bytes 2097152 | tf_op jit(solution)/shard_map/reshape | solution.py:69
  104.0 61.6 %reduce-scatter.2.cloned.1.call-done = f32[256,128]{1,0:T(8,128)} async-done(((f32[2048,128]{1,0:T(8,128)}), f32[256,128]{1,0:T(8,128)}) %reduce-scatter.2.cloned.1.call-update) | async-done | bytes 131088 | tf_op jit(solution)/shard_map/reduce_scatter | solution.py:68
  165.6 1.8 fusion.13
  167.3 3.3 %all-to-all-start.2 = ((bf16[4,64,128]{2,1,0:T(8,128)(2,1)}), bf16[4,64,128]{2,1,0:T(8,128)(2,1)S(1)}, u32[]{:S(2)}, u32[]{:S(2)}) async-start(bf16[4,64,128]{2,1,0:T(8,128)(2,1)} %bitcast.11), calls=%async_computation.3 | async-start | bytes 131072 | tf_op jit(solution)/shard_map/all_to_all | solution.py:73
  170.6 4.1 %all-to-all-done.2 = bf16[4,64,128]{2,1,0:T(8,128)(2,1)S(1)} async-done(((bf16[4,64,128]{2,1,0:T(8,128)(2,1)}), bf16[4,64,128]{2,1,0:T(8,128)(2,1)S(1)}, u32[]{:S(2)}, u32[]{:S(2)}) %all-to-all-start.2) | async-done | bytes 65568 | tf_op jit(solution)/shard_map/all_to_all | solution.py:73
  174.7 0.1 fusion.14
  174.8 0.7 fusion.16
  (20 shorter events, 0.1 us)
Async XLA Ops:
  6.5 9.6 %copy-start = (bf16[20,512,128]{2,1,0:T(8,128)(2,1)S(1)}, bf16[20,512,128]{2,1,0:T(8,128)(2,1)}, u32[]{:S(2)}) copy-start(bf16[20,512,128]{2,1,0:T(8,128)(2,1)} %param.16) | copy-start | bytes 7864324
  8.0 70.4 %all-to-all-start.1 = ((s32[8,1,1]{2,1,0:T(1,128)}), s32[8,1,1]{2,1,0:T(1,128)S(1)}, u32[]{:S(2)}, u32[]{:S(2)}) async-start(s32[8,1,1]{2,1,0:T(1,128)} %copy.24), calls=%async_computation.1 | async-start | bytes 8192 | tf_op jit(solution)/shard_map/all_to_all | solution.py:58
  78.4 12.4 %all-to-all-start = ((s32[8,1,32]{2,1,0:T(1,128)}), s32[8,1,32]{2,1,0:T(1,128)S(1)}, u32[]{:S(2)}, u32[]{:S(2)}) async-start(s32[8,1,32]{2,1,0:T(1,128)} %bitcast), calls=%async_computation | async-start | bytes 8192 | tf_op jit(solution)/shard_map/all_to_all | solution.py:57
  84.4 81.2 %reduce-scatter.2.cloned.1.call-start = ((), (), s32[]{:S(2)}) async-start(), calls=%async_computation.4 | async-start | bytes 1179648 | tf_op jit(solution)/shard_map/reduce_scatter | solution.py:68
  90.8 84.8 %copy-start.1 = (bf16[20,512,128]{2,1,0:T(8,128)(2,1)S(1)}, bf16[20,512,128]{2,1,0:T(8,128)(2,1)}, u32[]{:S(2)}) copy-start(bf16[20,512,128]{2,1,0:T(8,128)(2,1)} %param.16) | copy-start | bytes 7864324
  90.8 13.2 %copy-start.5 = (bf16[128]{0:T(256)(128)(2,1)S(1)}, bf16[128]{0:T(256)(128)(2,1)}, u32[]{:S(2)}) copy-start(bf16[128]{0:T(256)(128)(2,1)} %param.18) | copy-start | bytes 772
  90.8 74.8 %copy-start.2 = (bf16[256,512]{1,0:T(8,128)(2,1)S(1)}, bf16[256,512]{1,0:T(8,128)(2,1)}, u32[]{:S(2)}) copy-start(bf16[256,512]{1,0:T(8,128)(2,1)} %param.10) | copy-start | bytes 786436
  90.8 74.8 %copy-start.3 = (bf16[512,128]{1,0:T(8,128)(2,1)S(1)}, bf16[512,128]{1,0:T(8,128)(2,1)}, u32[]{:S(2)}) copy-start(bf16[512,128]{1,0:T(8,128)(2,1)} %param.17) | copy-start | bytes 393220
  90.8 79.8 %copy-start.4 = (bf16[512]{0:T(512)(128)(2,1)S(1)}, bf16[512]{0:T(512)(128)(2,1)}, u32[]{:S(2)}) copy-start(bf16[512]{0:T(512)(128)(2,1)} %param.19) | copy-start | bytes 3076
  167.3 7.4 %all-to-all-start.2 = ((bf16[4,64,128]{2,1,0:T(8,128)(2,1)}), bf16[4,64,128]{2,1,0:T(8,128)(2,1)S(1)}, u32[]{:S(2)}, u32[]{:S(2)}) async-start(bf16[4,64,128]{2,1,0:T(8,128)(2,1)} %bitcast.11), calls=%async_computation.3 | async-start | bytes 131072 | tf_op jit(solution)/shard_map/all_to_all | solution.py:73
Sparse Core Ops, SparseCore 0:
  104.1 61.4 reduce-scatter.1
where the time goes:
time: 184 us; the launch traced here: 182 us
  waiting for transfers between devices  71.7 us (39%)
  local copies, waits for them, and re-layouts  50.8 us (28%)
  matrix products  27.9 us (15%)
  starting transfers between devices  16.6 us (9%)
  between operations  13.5 us (7%)
  other arithmetic  1.89 us (1%)
    reduce_scatter x1, waiting for transfers between devices, per_device(): lax.psum_scatter(summed.reshape(receivers * blocks * BLK, columns), 'dp',...  61.6 us
    reshape x1, local copies, waits for them, and re-layouts, per_device(): transform_slots(lookup, lookup_rows, flat_tiles)  18.2 us
    dot_general x1, local copies, waits for them, and re-layouts, transform_slots(): jnp.einsum('nij,njc->nic', adj_tiles, chosen, preferred_element_type=jnp....  17.4 us
    dot_general x1, matrix products, transform_slots(): jnp.einsum('nij,njc->nic', adj_tiles, chosen, preferred_element_type=jnp....  13.2 us
    dot_general x1, matrix products, per_device(): jnp.einsum('rkb,rkx->rbx', weights, message, precision=lax.Precision.HIGH...  10 us
    gather x1, local copies, waits for them, and re-layouts, transform_slots(): chosen = jnp.take(lookup, lookup_rows, axis=0)  8.61 us
    all_to_all x1, starting transfers between devices, per_device(): lax.all_to_all(live_count.reshape(peer_count, 1), 'dp', split_axis=0, con...  7.28 us
    all_to_all x1, waiting for transfers between devices, per_device(): lax.all_to_all(target_block, 'dp', split_axis=0, concat_axis=0, tiled=True)  6.06 us
  transfers between devices with their start and end apart: 4, of which 3 were waited for; matrix products, arithmetic and copies ran while one was open for 35% of the time, Pallas kernels for 0%

commit v1 on v0

v1 whole, which is shorter than its diff:
```python
import jax
import jax.numpy as jnp
from jax import lax
from jax.experimental import pallas as pl
from jax.experimental.pallas import tpu as pltpu
from jax.sharding import PartitionSpec as P

epsilon = 1e-05


def group_of(count, most):
    return max(g for g in range(1, most + 1) if count % g == 0)


def table_kernel(features_ref, weight_ref, self_ref, bias_ref, table_ref, own_ref):
    step = pl.program_id(0)
    group, _, columns = weight_ref.shape
    side = table_ref.shape[1]
    blocks = features_ref.shape[0] // side
    rows = features_ref[...]

    @pl.when(step == 0)
    def _():
        own = jnp.dot(rows, self_ref[...], preferred_element_type=jnp.float32)
        own_ref[...] = own + bias_ref[...].astype(jnp.float32)
        table_ref[table_ref.shape[0] - 1] = jnp.zeros((side, columns), table_ref.dtype)

    wide = jnp.concatenate([weight_ref[g] for g in range(group)], axis=1)
    product = jnp.dot(rows, wide, preferred_element_type=jnp.float32).astype(table_ref.dtype)
    for g in range(group):
        for b in range(blocks):
            table_ref[(step * group + g) * blocks + b] = product[
                b * side : (b + 1) * side, g * columns : (g + 1) * columns
            ]


def message_kernel(me_ref, source_ref, type_ref, target_ref, tiles_ref, table_ref, own_ref, out_ref):
    step = pl.program_id(0)
    receivers, slots, side, _ = tiles_ref.shape
    columns = table_ref.shape[2]
    blocks = out_ref.shape[1] // side
    empty = table_ref.shape[0] - 1
    for d in range(receivers):
        receiver = step * receivers + d
        left = jnp.concatenate([tiles_ref[d, k] for k in range(slots)], axis=1)
        right = []
        for k in range(slots):
            row = type_ref[receiver, k] * blocks + source_ref[receiver, k]
            target = target_ref[receiver, k]
            picked = [table_ref[jnp.where(target == b, row, empty)] for b in range(blocks)]
            right.append(jnp.concatenate(picked, axis=1))
        total = jnp.dot(left, jnp.concatenate(right, axis=0), preferred_element_type=jnp.float32)
        mine = receiver == me_ref[0]
        for b in range(blocks):
            part = slice(b * side, (b + 1) * side)
            piece = total[:, b * columns : (b + 1) * columns]
            out_ref[d, part, :] = (piece + jnp.where(mine, own_ref[part, :], 0.0)).astype(out_ref.dtype)


def finish_kernel(parts_ref, gain_ref, out_ref):
    senders, pieces, rows, columns = parts_ref.shape
    hidden = []
    square = jnp.zeros((rows, 1), jnp.float32)
    for m in range(pieces):
        total = parts_ref[0, m].astype(jnp.float32)
        for s in range(1, senders):
            total = total + parts_ref[s, m].astype(jnp.float32)
        value = jnp.maximum(total, 0.0).astype(jnp.bfloat16).astype(jnp.float32)
        square = square + jnp.sum(value * value, axis=1, keepdims=True)
        hidden.append(value)
    scale = lax.rsqrt(square / (pieces * columns) + epsilon)
    for m in range(pieces):
        part = slice(m * columns, (m + 1) * columns)
        out_ref[:, part] = (hidden[m] * scale * gain_ref[:, part].astype(jnp.float32)).astype(out_ref.dtype)


def per_device(
    features,
    adjacency,
    source_block,
    edge_type,
    target_block,
    live_count,
    relation_weight,
    self_weight,
    layer_bias,
    norm_gain,
):
    peers = lax.axis_size("dp")
    splits = lax.axis_size("mp")
    slots = source_block.shape[1]
    side = adjacency.shape[2]
    node_rows, width = features.shape
    blocks = node_rows // side
    relations, _, columns = relation_weight.shape

    active = jnp.arange(slots, dtype=jnp.int32)[None, :] < live_count.reshape(peers, 1)
    routed = lax.all_to_all(
        jnp.where(active, target_block, blocks), "dp", split_axis=0, concat_axis=0, tiled=True
    )

    group = group_of(relations, 4)
    entries = relations * blocks + 1
    table, own = pl.pallas_call(
        table_kernel,
        grid=(relations // group,),
        in_specs=[
            pl.BlockSpec((node_rows, width), lambda i: (0, 0)),
            pl.BlockSpec((group, width, columns), lambda i: (i, 0, 0)),
            pl.BlockSpec((width, columns), lambda i: (0, 0)),
            pl.BlockSpec((1, columns), lambda i: (0, 0)),
        ],
        out_specs=[
            pl.BlockSpec((entries, side, columns), lambda i: (0, 0, 0)),
            pl.BlockSpec((node_rows, columns), lambda i: (0, 0)),
        ],
        out_shape=[
            jax.ShapeDtypeStruct((entries, side, columns), jnp.bfloat16),
            jax.ShapeDtypeStruct((node_rows, columns), jnp.float32),
        ],
        cost_estimate=pl.CostEstimate(
            flops=2 * node_rows * width * columns * (relations + 1),
            bytes_accessed=2 * (relations * width * columns + entries * side * columns),
            transcendentals=0,
        ),
        name="relation_table",
    )(features, relation_weight, self_weight, layer_bias.reshape(1, columns))

    together = group_of(peers, max(1, 32 // slots))
    smem = pl.BlockSpec(memory_space=pltpu.SMEM)
    partial = pl.pallas_call(
        message_kernel,
        grid=(peers // together,),
        in_specs=[
            smem,
            smem,
            smem,
            smem,
            pl.BlockSpec((together, slots, side, side), lambda i: (i, 0, 0, 0)),
            pl.BlockSpec((entries, side, columns), lambda i: (0, 0, 0)),
            pl.BlockSpec((node_rows, columns), lambda i: (0, 0)),
        ],
        out_specs=pl.BlockSpec((together, node_rows, columns), lambda i: (i, 0, 0)),
        out_shape=jax.ShapeDtypeStruct((peers, node_rows, columns), jnp.bfloat16),
        cost_estimate=pl.CostEstimate(
            flops=2 * peers * slots * side * side * columns * blocks,
            bytes_accessed=2 * (peers * slots * side * side + peers * node_rows * columns),
            transcendentals=0,
        ),
        name="slot_messages",
    )(
        lax.axis_index("dp").astype(jnp.int32).reshape(1),
        source_block,
        edge_type,
        routed,
        adjacency,
        table,
        own,
    )

    arrived = lax.all_to_all(
        partial.reshape(peers * node_rows, columns),
        ("dp", "mp"),
        split_axis=0,
        concat_axis=0,
        tiled=True,
    )
    rows = node_rows // splits
    return pl.pallas_call(
        finish_kernel,
        out_shape=jax.ShapeDtypeStruct((rows, splits * columns), jnp.bfloat16),
        name="sum_and_norm",
    )(arrived.reshape(peers, splits, rows, columns), norm_gain.reshape(1, splits * columns))


def solution(mesh):
    return jax.shard_map(
        per_device,
        mesh=mesh,
        in_specs=(
            P("dp", None),
            P("dp", None, None, None),
            P("dp", None),
            P("dp", None),
            P("dp", None),
            P("dp", None),
            P(None, None, "mp"),
            P(None, "mp"),
            P("mp"),
            P(),
        ),
        out_specs=P(("dp", "mp"), None),
        check_vma=False,
    )
```

time: 184 us -> 48.3 us (0.26)
  waiting for transfers between devices: 71.7 us -> 15.9 us
  local copies, waits for them, and re-layouts: 50.8 us -> 1.93 us
  matrix products: 27.9 us -> 0 us
  Pallas kernels: 0 us -> 16.1 us
  between operations: 13.5 us -> 0.02 us
  starting transfers between devices: 16.6 us -> 12.4 us
    reduce_scatter x1 -> x0, waiting for transfers between devices: 61.6 us -> none  [per_device(): lax.psum_scatter(summed.reshape(receivers * blocks * BLK, columns), 'dp',...]
    dot_general x4 -> x0, matrix products: 27.9 us -> none  [the longest x1 13.2 us: transform_slots(): jnp.einsum('nij,njc->nic', adj_tiles, chosen, preferred_element_type=jnp....]
    reshape x4 -> x1, local copies, waits for them, and re-layouts: 21.5 us -> 0.55 us  [per_device(): norm_gain.reshape(1, splits * columns)]
    dot_general x1 -> x0, local copies, waits for them, and re-layouts: 17.4 us -> none  [transform_slots(): jnp.einsum('nij,njc->nic', adj_tiles, chosen, preferred_element_type=jnp....]
    pallas_call x0 -> x3, Pallas kernels: none -> 16.1 us  [the longest x1 8.74 us: per_device(): pl.pallas_call(message_kernel, grid=(peers // together,), in_specs=[smem,...]
    gather x1 -> x0, local copies, waits for them, and re-layouts: 8.61 us -> none  [transform_slots(): chosen = jnp.take(lookup, lookup_rows, axis=0)]
    all_to_all x3 -> x2, waiting for transfers between devices: 10.1 us -> 15.9 us  [the longest x1 15.1 us: per_device(): lax.all_to_all(partial.reshape(peers * node_rows, columns), ('dp', 'mp'),...]
    all_to_all x3 -> x2, starting transfers between devices: 16.6 us -> 12.4 us  [the longest x1 7.28 us: per_device(): lax.all_to_all(jnp.where(active, target_block, blocks), 'dp', split_axis=...]
  transfers between devices with their start and end apart: 4 -> 2, of which waited for: 3 -> 2; matrix products, arithmetic and copies ran while one was open for 35% -> 1% of each run, Pallas kernels for 0% -> 12%
where the time goes in v1:
time: 48.3 us; the launch traced here: 47.8 us
  Pallas kernels  16.1 us (33%)
  waiting for transfers between devices  15.9 us (33%)
  starting transfers between devices  12.4 us (26%)
  local copies, waits for them, and re-layouts  1.93 us (4%)
  other arithmetic  1.35 us (3%)
    all_to_all x1, waiting for transfers between devices, per_device(): lax.all_to_all(partial.reshape(peers * node_rows, columns), ('dp', 'mp'),...  15.1 us
    pallas_call x1, Pallas kernels, per_device(): pl.pallas_call(message_kernel, grid=(peers // together,), in_specs=[smem,...  8.74 us
    all_to_all x1, starting transfers between devices, per_device(): lax.all_to_all(jnp.where(active, target_block, blocks), 'dp', split_axis=...  7.28 us
    pallas_call x1, Pallas kernels, per_device(): pl.pallas_call(table_kernel, grid=(relations // group,), in_specs=[pl.Blo...  5.54 us
    all_to_all x1, starting transfers between devices, per_device(): lax.all_to_all(partial.reshape(peers * node_rows, columns), ('dp', 'mp'),...  5.16 us
    pallas_call x1, Pallas kernels, per_device(): pl.pallas_call(finish_kernel, out_shape=jax.ShapeDtypeStruct((rows, split...  1.85 us
    unnamed x6, local copies, waits for them, and re-layouts  1.39 us
    select_n x1, other arithmetic, per_device(): jnp.where(active, target_block, blocks)  1.35 us
  transfers between devices with their start and end apart: 2, of which 2 were waited for; matrix products, arithmetic and copies ran while one was open for 1% of the time, Pallas kernels for 12%

profile of v1, /device:TPU:0, one launch (start us, length us, event | category | flops | bytes accessed | tf_op | source)
XLA Modules:
  0.0 47.8 jit_solution(5466610212973248303)
XLA Ops:
  0.0 1.4 %fusion = s32[8,32]{1,0:T(8,128)} fusion(s32[8,32]{1,0:T(8,128)} %param.14, s32[8]{0:T(128)} %bitcast.11), kind=kLoop, calls=%fused_computation.1 | loop fusion | flops 512 | bytes 2080 | tf_op jit(solution)/shard_map/jit(_where)/select_n | solution.py:99
  1.4 7.3 %all-to-all-start = ((s32[8,1,32]{2,1,0:T(1,128)}), s32[8,1,32]{2,1,0:T(1,128)S(1)}, u32[]{:S(2)}, u32[]{:S(2)}) async-start(s32[8,1,32]{2,1,0:T(1,128)} %bitcast.2), calls=%async_computation | async-start | bytes 8192 | tf_op jit(solution)/shard_map/all_to_all | solution.py:98
  8.6 5.5 %relation_table.1 = (bf16[41,128,128]{2,1,0:T(8,128)(2,1)}, f32[256,128]{1,0:T(8,128)}) custom-call(bf16[256,512]{1,0:T(8,128)(2,1)} %features_ref.1, bf16[20,512,128]{2,1,0:T(8,128)(2,1)} %weight_ref.1, bf16[512,128]{1,0:T(8,128)(2,1)} %self_ref.1, bf16[1,128]{1,0:T(2,128)(2,1)} %bitcast.10), custom_call_target="tpu_custom_call" | custom-call | flops 704643072 | bytes 3964928 | tf_op jit(solution)/shard_map/relation_table/pallas_call | solution.py:104
  14.2 0.9 %all-to-all-done = s32[8,1,32]{2,1,0:T(1,128)S(1)} async-done(((s32[8,1,32]{2,1,0:T(1,128)}), s32[8,1,32]{2,1,0:T(1,128)S(1)}, u32[]{:S(2)}, u32[]{:S(2)}) %all-to-all-start) | async-done | bytes 1056 | tf_op jit(solution)/shard_map/all_to_all | solution.py:98
  15.1 0.0 copy-start.1
  15.1 0.6 %copy-done.1 = s32[8,1,32]{2,1,0:T(1,128)} copy-done((s32[8,1,32]{2,1,0:T(1,128)}, s32[8,1,32]{2,1,0:T(1,128)S(1)}, u32[]{:S(2)}) %copy-start.1) | copy-done | bytes 1048
  15.6 0.0 copy-start.2
  15.6 8.7 %slot_messages.1 = bf16[8,256,128]{2,1,0:T(8,128)(2,1)} custom-call(s32[1]{0:T(128)} %bitcast.me_ref, s32[8,32]{1,0:T(8,128)} %source_ref.1, s32[8,32]{1,0:T(8,128)} %type_ref.1, s32[8,32]{1,0:T(8,128)} %bitcast.9, bf16[8,32,128,128]{3,2,1,0:T(8,128)(2,1)} %tiles_ref.1, bf16[41,128,128]{2,1,0:T(8,128)(2,1)} %get-tuple-element.7.table_ref, ...), custom_call_target="tpu_custom_call" | custom-call | flops 2147483648 | bytes 8912896 | tf_op jit(solution)/shard_map/slot_messages/pallas_call | solution.py:131
  24.4 5.2 %all-to-all-start.1 = ((bf16[32,64,128]{2,1,0:T(8,128)(2,1)}), bf16[32,64,128]{2,1,0:T(8,128)(2,1)S(1)}, u32[]{:S(2)}, u32[]{:S(2)}) async-start(bf16[32,64,128]{2,1,0:T(8,128)(2,1)} %bitcast.7), calls=%async_computation.1 | async-start | bytes 1048576 | tf_op jit(solution)/shard_map/all_to_all | solution.py:161
  29.6 0.0 copy-done.2
  29.6 0.5 %reshape.24.gain_ref = bf16[1,512]{1,0:T(2,128)(2,1)} reshape(bf16[512]{0:T(512)(128)(2,1)S(1)} %copy-done.2) | data formatting | bytes 2048 | tf_op jit(solution)/shard_map/reshape | solution.py:173
  30.1 15.1 %all-to-all-done.1 = bf16[32,64,128]{2,1,0:T(8,128)(2,1)S(1)} async-done(((bf16[32,64,128]{2,1,0:T(8,128)(2,1)}), bf16[32,64,128]{2,1,0:T(8,128)(2,1)S(1)}, u32[]{:S(2)}, u32[]{:S(2)}) %all-to-all-start.1) | async-done | bytes 524320 | tf_op jit(solution)/shard_map/all_to_all | solution.py:161
  45.2 0.0 copy-start
  45.2 0.8 %copy-done = bf16[32,64,128]{2,1,0:T(8,128)(2,1)} copy-done((bf16[32,64,128]{2,1,0:T(8,128)(2,1)}, bf16[32,64,128]{2,1,0:T(8,128)(2,1)S(1)}, u32[]{:S(2)}) %copy-start) | copy-done | bytes 524312
  46.0 1.8 %sum_and_norm.1 = bf16[64,512]{1,0:T(8,128)(2,1)} custom-call(bf16[8,4,64,128]{3,2,1,0:T(8,128)(2,1)} %bitcast.8, bf16[1,512]{1,0:T(2,128)(2,1)} %reshape.24.gain_ref), custom_call_target="tpu_custom_call" | custom-call | tf_op jit(solution)/shard_map/sum_and_norm/pallas_call | solution.py:169
Async XLA Ops:
  1.4 13.7 %all-to-all-start = ((s32[8,1,32]{2,1,0:T(1,128)}), s32[8,1,32]{2,1,0:T(1,128)S(1)}, u32[]{:S(2)}, u32[]{:S(2)}) async-start(s32[8,1,32]{2,1,0:T(1,128)} %bitcast.2), calls=%async_computation | async-start | bytes 8192 | tf_op jit(solution)/shard_map/all_to_all | solution.py:98
  15.1 0.6 %copy-start.1 = (s32[8,1,32]{2,1,0:T(1,128)}, s32[8,1,32]{2,1,0:T(1,128)S(1)}, u32[]{:S(2)}) copy-start(s32[8,1,32]{2,1,0:T(1,128)S(1)} %all-to-all-done) | copy-start | bytes 3076
  15.6 13.9 %copy-start.2 = (bf16[512]{0:T(512)(128)(2,1)S(1)}, bf16[512]{0:T(512)(128)(2,1)}, u32[]{:S(2)}) copy-start(bf16[512]{0:T(512)(128)(2,1)} %param.19) | copy-start | bytes 3076
  24.4 20.8 %all-to-all-start.1 = ((bf16[32,64,128]{2,1,0:T(8,128)(2,1)}), bf16[32,64,128]{2,1,0:T(8,128)(2,1)S(1)}, u32[]{:S(2)}, u32[]{:S(2)}) async-start(bf16[32,64,128]{2,1,0:T(8,128)(2,1)} %bitcast.7), calls=%async_computation.1 | async-start | bytes 1048576 | tf_op jit(solution)/shard_map/all_to_all | solution.py:161
  45.2 0.8 %copy-start = (bf16[32,64,128]{2,1,0:T(8,128)(2,1)}, bf16[32,64,128]{2,1,0:T(8,128)(2,1)S(1)}, u32[]{:S(2)}) copy-start(bf16[32,64,128]{2,1,0:T(8,128)(2,1)S(1)} %all-to-all-done.1) | copy-start | bytes 1572868

commit v2 on v1

v2 whole, which is shorter than its diff:
```python
import jax
import jax.numpy as jnp
from jax import lax
from jax.experimental import pallas as pl
from jax.experimental.pallas import tpu as pltpu
from jax.sharding import PartitionSpec as P

epsilon = 1e-05
UNROLL = 1
SCRATCH_BYTES = 20 * 1024 * 1024


def on_chip(array):
    return pltpu.with_memory_space_constraint(array, pltpu.VMEM)


def off_chip(array):
    return pltpu.with_memory_space_constraint(array, pltpu.HBM)


def group_of(count, most):
    return max(g for g in range(1, most + 1) if count % g == 0)


def table_kernel(
    features_hbm, weight_hbm, tiles_hbm, table_ref, early_ref,
    features_ref, weight_ref, few_sems, weight_sems,
):
    relations, _, columns = weight_ref.shape
    side = table_ref.shape[1]
    blocks = features_ref.shape[0] // side
    group = group_of(relations, 2)
    chunks = relations // group
    early = early_ref.shape[0]

    halves = 2 if chunks % 2 == 0 else 1
    per_half = chunks // halves

    def weight_copy(half):
        part = pl.ds(half * per_half * group, per_half * group)
        return pltpu.make_async_copy(weight_hbm.at[part], weight_ref.at[part], weight_sems.at[half])

    rows_copy = pltpu.make_async_copy(features_hbm, features_ref, few_sems.at[0])
    early_copy = pltpu.make_async_copy(tiles_hbm.at[pl.ds(0, early)], early_ref, few_sems.at[1])
    rows_copy.start()
    for half in range(halves):
        weight_copy(half).start()
    early_copy.start()
    table_ref[table_ref.shape[0] - 1] = jnp.zeros((side, columns), table_ref.dtype)
    rows_copy.wait()

    def some_relations(step, carry):
        first = step * group
        wide = jnp.concatenate([weight_ref[first + g] for g in range(group)], axis=1)
        product = jnp.dot(features_ref[...], wide, preferred_element_type=jnp.float32)
        product = product.astype(table_ref.dtype)
        for g in range(group):
            for b in range(blocks):
                table_ref[(first + g) * blocks + b] = product[
                    b * side : (b + 1) * side, g * columns : (g + 1) * columns
                ]
        return carry

    for half in range(halves):
        weight_copy(half).wait()
        bounds = (half * per_half, (half + 1) * per_half)
        lax.fori_loop(*bounds, some_relations, 0, unroll=group_of(per_half, 5))
    early_copy.wait()


def message_kernel(
    me_ref, source_ref, type_ref, target_ref, early_ref, tiles_hbm, table_ref,
    features_hbm, self_hbm, bias_hbm, out_ref,
    late_ref, features_ref, self_ref, bias_ref, mine_ref, tile_sems, few_sems,
):
    early, slots, side, _ = early_ref.shape
    receivers = out_ref.shape[0]
    late = receivers - early
    columns = table_ref.shape[2]
    blocks = out_ref.shape[1] // side
    empty = table_ref.shape[0] - 1

    cuts = [0, late - late // 2, late]
    waves = [(cuts[i], cuts[i + 1] - cuts[i]) for i in range(2) if cuts[i + 1] > cuts[i]]

    def wave_copy(wave):
        start, count = waves[wave]
        return pltpu.make_async_copy(
            tiles_hbm.at[pl.ds(early + start, count)], late_ref.at[pl.ds(start, count)], tile_sems.at[wave]
        )

    few = [
        pltpu.make_async_copy(features_hbm, features_ref, few_sems.at[0]),
        pltpu.make_async_copy(self_hbm, self_ref, few_sems.at[1]),
        pltpu.make_async_copy(bias_hbm, bias_ref, few_sems.at[2]),
    ]

    def one_receiver(receiver, tiles_ref, place):
        left = jnp.concatenate([tiles_ref[place, k] for k in range(slots)], axis=1)
        right = []
        for k in range(slots):
            row = type_ref[receiver, k] * blocks + source_ref[receiver, k]
            target = target_ref[receiver, k]
            picked = [table_ref[jnp.where(target == b, row, empty)] for b in range(blocks)]
            right.append(jnp.concatenate(picked, axis=1))
        total = jnp.dot(left, jnp.concatenate(right, axis=0), preferred_element_type=jnp.float32)
        for b in range(blocks):
            part = slice(b * side, (b + 1) * side)
            out_ref[receiver, part, :] = total[:, b * columns : (b + 1) * columns].astype(out_ref.dtype)
        mine_ref[jnp.where(receiver == me_ref[0], 0, 1)] = total

    def first_ones(place, carry):
        one_receiver(place, early_ref, place)
        return carry

    def other_ones(place, carry):
        one_receiver(early + place, late_ref, place)
        return carry

    wave_copy(0).start()
    lax.fori_loop(0, early, first_ones, 0, unroll=group_of(early, UNROLL))
    for wave in range(1, len(waves)):
        wave_copy(wave).start()
    for copy in few:
        copy.start()
    for wave, (start, count) in enumerate(waves):
        wave_copy(wave).wait()
        lax.fori_loop(start, start + count, other_ones, 0, unroll=group_of(count, UNROLL))
    for copy in few:
        copy.wait()
    own = jnp.dot(features_ref[...], self_ref[...], preferred_element_type=jnp.float32)
    own = own + bias_ref[...].astype(jnp.float32)
    for b in range(blocks):
        part = slice(b * side, (b + 1) * side)
        piece = mine_ref[0, :, b * columns : (b + 1) * columns]
        out_ref[me_ref[0], part, :] = (own[part, :] + piece).astype(out_ref.dtype)


def finish_kernel(parts_ref, gain_ref, out_ref):
    senders, pieces, rows, columns = parts_ref.shape
    hidden = []
    square = jnp.zeros((rows, 1), jnp.float32)
    for m in range(pieces):
        total = parts_ref[0, m].astype(jnp.float32)
        for s in range(1, senders):
            total = total + parts_ref[s, m].astype(jnp.float32)
        value = jnp.maximum(total, 0.0).astype(jnp.bfloat16).astype(jnp.float32)
        square = square + jnp.sum(value * value, axis=1, keepdims=True)
        hidden.append(value)
    scale = lax.rsqrt(square / (pieces * columns) + epsilon)
    for m in range(pieces):
        part = slice(m * columns, (m + 1) * columns)
        out_ref[:, part] = (hidden[m] * scale * gain_ref[:, part].astype(jnp.float32)).astype(out_ref.dtype)


def per_device(
    features,
    adjacency,
    source_block,
    edge_type,
    target_block,
    live_count,
    relation_weight,
    self_weight,
    layer_bias,
    norm_gain,
):
    peers = lax.axis_size("dp")
    splits = lax.axis_size("mp")
    slots = source_block.shape[1]
    side = adjacency.shape[2]
    node_rows, width = features.shape
    blocks = node_rows // side
    relations, _, columns = relation_weight.shape

    active = jnp.arange(slots, dtype=jnp.int32)[None, :] < live_count.reshape(peers, 1)
    routed = lax.all_to_all(
        jnp.where(active, target_block, blocks), "dp", split_axis=0, concat_axis=0, tiled=True
    )

    entries = relations * blocks + 1
    early = max(1, peers // 4)
    vmem = pl.BlockSpec(memory_space=pltpu.VMEM)
    smem = pl.BlockSpec(memory_space=pltpu.SMEM)
    hbm = pl.BlockSpec(memory_space=pltpu.HBM)
    params = pltpu.CompilerParams(vmem_limit_bytes=SCRATCH_BYTES)
    table, early_tiles = pl.pallas_call(
        table_kernel,
        in_specs=[hbm] * 3,
        out_specs=[vmem] * 2,
        out_shape=[
            pltpu.VMEM((entries, side, columns), jnp.bfloat16),
            pltpu.VMEM((early, slots, side, side), jnp.bfloat16),
        ],
        scratch_shapes=[
            pltpu.VMEM((node_rows, width), jnp.bfloat16),
            pltpu.VMEM((relations, width, columns), jnp.bfloat16),
            pltpu.SemaphoreType.DMA((2,)),
            pltpu.SemaphoreType.DMA((2,)),
        ],
        cost_estimate=pl.CostEstimate(
            flops=2 * node_rows * width * columns * relations,
            bytes_accessed=2 * (relations * width * columns + early * slots * side * side),
            transcendentals=0,
        ),
        compiler_params=params,
        name="relation_table",
    )(*map(off_chip, (features, relation_weight, adjacency)))

    partial = pl.pallas_call(
        message_kernel,
        in_specs=[smem] * 4 + [vmem, hbm, vmem, hbm, hbm, hbm],
        out_specs=vmem,
        out_shape=jax.ShapeDtypeStruct((peers, node_rows, columns), jnp.bfloat16),
        scratch_shapes=[
            pltpu.VMEM((peers - early, slots, side, side), jnp.bfloat16),
            pltpu.VMEM((node_rows, width), jnp.bfloat16),
            pltpu.VMEM((width, columns), jnp.bfloat16),
            pltpu.VMEM((1, columns), jnp.bfloat16),
            pltpu.VMEM((2, side, blocks * columns), jnp.float32),
            pltpu.SemaphoreType.DMA((2,)),
            pltpu.SemaphoreType.DMA((3,)),
        ],
        cost_estimate=pl.CostEstimate(
            flops=2 * peers * slots * side * side * columns * blocks,
            bytes_accessed=2 * ((peers - early) * slots * side * side + peers * node_rows * columns),
            transcendentals=0,
        ),
        compiler_params=params,
        name="slot_messages",
    )(
        lax.axis_index("dp").astype(jnp.int32).reshape(1),
        source_block,
        edge_type,
        routed,
        on_chip(early_tiles),
        off_chip(adjacency),
        on_chip(table),
        *map(off_chip, (features, self_weight, layer_bias.reshape(1, columns))),
    )

    arrived = lax.all_to_all(
        partial.reshape(peers * node_rows, columns),
        ("dp", "mp"),
        split_axis=0,
        concat_axis=0,
        tiled=True,
    )
    rows = node_rows // splits
    return pl.pallas_call(
        finish_kernel,
        out_shape=jax.ShapeDtypeStruct((rows, splits * columns), jnp.bfloat16),
        compiler_params=params,
        name="sum_and_norm",
    )(on_chip(arrived.reshape(peers, splits, rows, columns)), norm_gain.reshape(1, splits * columns))


def solution(mesh):
    return jax.shard_map(
        per_device,
        mesh=mesh,
        in_specs=(
            P("dp", None),
            P("dp", None, None, None),
            P("dp", None),
            P("dp", None),
            P("dp", None),
            P("dp", None),
            P(None, None, "mp"),
            P(None, "mp"),
            P("mp"),
            P(),
        ),
        out_specs=P(("dp", "mp"), None),
        check_vma=False,
    )
```

time: 48.3 us -> 40.9 us (0.85)
  Pallas kernels: 16.1 us -> 9.81 us
  waiting for transfers between devices: 15.9 us -> 19.4 us
  starting transfers between devices: 12.4 us -> 9.9 us
  local copies, waits for them, and re-layouts: 1.93 us -> 0.02 us
    pallas_call x2, Pallas kernels: 14.3 us -> 9.01 us  [the longest x1 6.4 us: per_device(): pl.pallas_call(message_kernel, in_specs=[smem] * 4 + [vmem, hbm, vmem, hb...]
    all_to_all x1, waiting for transfers between devices: 0.87 us -> 3.78 us  [per_device(): lax.all_to_all(jnp.where(active, target_block, blocks), 'dp', split_axis=...]
    all_to_all x1, starting transfers between devices: 5.16 us -> 2.62 us  [per_device(): lax.all_to_all(partial.reshape(peers * node_rows, columns), ('dp', 'mp'),...]
    unnamed x6, local copies, waits for them, and re-layouts: 1.39 us -> 0.01 us
    pallas_call x1, Pallas kernels: 1.85 us -> 0.81 us  [per_device(): pl.pallas_call(finish_kernel, out_shape=jax.ShapeDtypeStruct((rows, split...]
    reshape x1, local copies, waits for them, and re-layouts: 0.55 us -> 0.01 us  [per_device(): norm_gain.reshape(1, splits * columns)]
    all_to_all x1, waiting for transfers between devices: 15.1 us -> 15.6 us  [per_device(): lax.all_to_all(partial.reshape(peers * node_rows, columns), ('dp', 'mp'),...]
  transfers between devices with their start and end apart: 2 -> 2, of which waited for: 2 -> 2; matrix products, arithmetic and copies ran while one was open for 1% -> 0% of each run, Pallas kernels for 12% -> 6%
where the time goes in v2:
time: 40.9 us; the launch traced here: 40.5 us
  waiting for transfers between devices  19.4 us (47%)
  starting transfers between devices  9.9 us (24%)
  Pallas kernels  9.81 us (24%)
  other arithmetic  1.35 us (3%)
    all_to_all x1, waiting for transfers between devices, per_device(): lax.all_to_all(partial.reshape(peers * node_rows, columns), ('dp', 'mp'),...  15.6 us
    all_to_all x1, starting transfers between devices, per_device(): lax.all_to_all(jnp.where(active, target_block, blocks), 'dp', split_axis=...  7.28 us
    pallas_call x1, Pallas kernels, per_device(): pl.pallas_call(message_kernel, in_specs=[smem] * 4 + [vmem, hbm, vmem, hb...  6.4 us
    all_to_all x1, waiting for transfers between devices, per_device(): lax.all_to_all(jnp.where(active, target_block, blocks), 'dp', split_axis=...  3.78 us
    all_to_all x1, starting transfers between devices, per_device(): lax.all_to_all(partial.reshape(peers * node_rows, columns), ('dp', 'mp'),...  2.62 us
    pallas_call x1, Pallas kernels, per_device(): pl.pallas_call(table_kernel, in_specs=[hbm] * 3, out_specs=[vmem] * 2, ou...  2.61 us
    select_n x1, other arithmetic, per_device(): jnp.where(active, target_block, blocks)  1.35 us
  transfers between devices with their start and end apart: 2, of which 2 were waited for; matrix products, arithmetic and copies ran while one was open for 0% of the time, Pallas kernels for 6%

profile of v2, /device:TPU:0, one launch (start us, length us, event | category | flops | bytes accessed | tf_op | source)
XLA Modules:
  0.0 40.5 jit_solution(596035785808140245)
XLA Ops:
  0.0 1.4 %fusion = s32[8,32]{1,0:T(8,128)} fusion(s32[8,32]{1,0:T(8,128)} %param.14, s32[8]{0:T(128)} %bitcast.10), kind=kLoop, calls=%fused_computation.1 | loop fusion | flops 512 | bytes 2080 | tf_op jit(solution)/shard_map/jit(_where)/select_n | solution.py:178
  1.4 7.3 %all-to-all-start = ((s32[8,1,32]{2,1,0:T(1,128)}), s32[8,1,32]{2,1,0:T(1,128)S(1)}, u32[]{:S(2)}, u32[]{:S(2)}) async-start(s32[8,1,32]{2,1,0:T(1,128)} %bitcast.2), calls=%async_computation | async-start | bytes 8192 | tf_op jit(solution)/shard_map/all_to_all | solution.py:177
  8.6 0.0 copy-start
  8.6 0.0 copy-start.1
  8.6 2.6 %relation_table.1 = (bf16[41,128,128]{2,1,0:T(8,128)(2,1)S(1)}, bf16[2,32,128,128]{3,2,1,0:T(8,128)(2,1)S(1)}) custom-call(bf16[256,512]{1,0:T(8,128)(2,1)} %features_hbm.3, bf16[20,512,128]{2,1,0:T(8,128)(2,1)} %weight_hbm.1, bf16[8,32,128,128]{3,2,1,0:T(8,128)(2,1)} %tiles_hbm.3), custom_call_target="tpu_custom_call" | custom-call | flops 671088640 | bytes 4718592 | tf_op jit(solution)/shard_map/relation_table/pallas_call | solution.py:187
  11.3 3.8 %all-to-all-done = s32[8,1,32]{2,1,0:T(1,128)S(1)} async-done(((s32[8,1,32]{2,1,0:T(1,128)}), s32[8,1,32]{2,1,0:T(1,128)S(1)}, u32[]{:S(2)}, u32[]{:S(2)}) %all-to-all-start) | async-done | bytes 1056 | tf_op jit(solution)/shard_map/all_to_all | solution.py:177
  15.1 0.0 copy-done
  15.1 0.0 copy-done.1
  15.1 0.0 copy-start.2
  15.1 6.4 %slot_messages.1 = bf16[8,256,128]{2,1,0:T(8,128)(2,1)} custom-call(s32[1]{0:T(128)} %bitcast.me_ref, s32[8,32]{1,0:T(8,128)S(1)} %copy-done, s32[8,32]{1,0:T(8,128)S(1)} %copy-done.1, s32[8,32]{1,0:T(8,128)S(1)} %bitcast.8, bf16[2,32,128,128]{3,2,1,0:T(8,128)(2,1)S(1)} %get-tuple-element.7.early_ref, bf16[8,32,128,128]{3,2,1,0:T(8,128)(2,1)} %tiles_hbm.3, ...), custom_call_target="tpu_custom_call" | custom-call | flops 2147483648 | bytes 6815744 | tf_op jit(solution)/shard_map/slot_messages/pallas_call | solution.py:210
  21.5 2.6 %all-to-all-start.1 = ((bf16[32,64,128]{2,1,0:T(8,128)(2,1)}), bf16[32,64,128]{2,1,0:T(8,128)(2,1)S(1)}, u32[]{:S(2)}, u32[]{:S(2)}) async-start(bf16[32,64,128]{2,1,0:T(8,128)(2,1)} %bitcast.5), calls=%async_computation.1 | async-start | bytes 1048576 | tf_op jit(solution)/shard_map/all_to_all | solution.py:242
  24.1 0.0 copy-done.2
  24.1 15.6 %all-to-all-done.1 = bf16[32,64,128]{2,1,0:T(8,128)(2,1)S(1)} async-done(((bf16[32,64,128]{2,1,0:T(8,128)(2,1)}), bf16[32,64,128]{2,1,0:T(8,128)(2,1)S(1)}, u32[]{:S(2)}, u32[]{:S(2)}) %all-to-all-start.1) | async-done | bytes 524320 | tf_op jit(solution)/shard_map/all_to_all | solution.py:242
  39.7 0.8 %sum_and_norm.1 = bf16[64,512]{1,0:T(8,128)(2,1)} custom-call(bf16[8,4,64,128]{3,2,1,0:T(8,128)(2,1)S(1)} %bitcast.7, bf16[1,512]{1,0:T(2,128)(2,1)S(1)} %reshape.24.gain_ref), custom_call_target="tpu_custom_call" | custom-call | tf_op jit(solution)/shard_map/sum_and_norm/pallas_call | solution.py:250
  (1 shorter events, 0.0 us)
Async XLA Ops:
  1.4 13.7 %all-to-all-start = ((s32[8,1,32]{2,1,0:T(1,128)}), s32[8,1,32]{2,1,0:T(1,128)S(1)}, u32[]{:S(2)}, u32[]{:S(2)}) async-start(s32[8,1,32]{2,1,0:T(1,128)} %bitcast.2), calls=%async_computation | async-start | bytes 8192 | tf_op jit(solution)/shard_map/all_to_all | solution.py:177
  8.6 6.4 %copy-start = (s32[8,32]{1,0:T(8,128)S(1)}, s32[8,32]{1,0:T(8,128)}, u32[]{:S(2)}) copy-start(s32[8,32]{1,0:T(8,128)} %source_ref.1) | copy-start | bytes 3076
  8.6 6.4 %copy-start.1 = (s32[8,32]{1,0:T(8,128)S(1)}, s32[8,32]{1,0:T(8,128)}, u32[]{:S(2)}) copy-start(s32[8,32]{1,0:T(8,128)} %type_ref.1) | copy-start | bytes 3076
  15.1 9.0 %copy-start.2 = (bf16[512]{0:T(512)(128)(2,1)S(1)}, bf16[512]{0:T(512)(128)(2,1)}, u32[]{:S(2)}) copy-start(bf16[512]{0:T(512)(128)(2,1)} %param.19) | copy-start | bytes 3076
  21.5 18.2 %all-to-all-start.1 = ((bf16[32,64,128]{2,1,0:T(8,128)(2,1)}), bf16[32,64,128]{2,1,0:T(8,128)(2,1)S(1)}, u32[]{:S(2)}, u32[]{:S(2)}) async-start(bf16[32,64,128]{2,1,0:T(8,128)(2,1)} %bitcast.5), calls=%async_computation.1 | async-start | bytes 1048576 | tf_op jit(solution)/shard_map/all_to_all | solution.py:242
